TPU v7x, 32 devices: a whole 2x2x4 slice. The times are simulated.
32 devices in a mesh: row: 8 (over y, x, core), shift: 4 (over z).
Axes of the slice: x: 2, y: 2, z: 4, core: 2. Of those that a mesh axis runs over, the one named last changes fastest.
Arguments:
- snapshots: bfloat16 [4096, 2, 128], P('row'), may hold values from -6 to 6
- tail_sensors: bfloat16 [128, 2, 128], replicated, may hold values from -6 to 6
- shift_offsets: int32 [12], P('shift'), may hold values from 0 to 128
- start_basis: float32 [64, 4096], P(None, 'row'), may hold values from -0.09375 to 0.09375
Outputs:
- covariance: float32 [4096, 4096], P('row', 'shift')
- signal_basis: float32 [64, 4096], P(None, 'row')
Inputs may be any that keep to these rules, and one draw needn't show every extreme that they name: `shift_offsets`: each shift's first sensor.
All inputs are finite; a program needn't handle non-finite values.
Results may differ from a plain program's by a relative error of at most 0.0031.
Values may be sent and summed in bfloat16 or wider, within the bound.
A program may use at most 64 MiB of HBM per device.

v0:
```python
import jax
import jax.numpy as jnp
from jax import lax
from jax.sharding import PartitionSpec as P

M = 4096
SNAPS = 128
ITERS = 2
half_root = 0.7071067811865476


def make_some(extended, offset, start, count):
    window = lax.dynamic_slice_in_dim(extended, offset + start, count, 0).astype(jnp.float32)
    mirror = lax.dynamic_slice_in_dim(extended, offset + M - start - count, count, 0).astype(
        jnp.float32
    )[::-1]
    summed_pair = window + mirror
    difference = window - mirror
    upper_rows = jnp.concatenate([summed_pair[:, 0], summed_pair[:, 1]], axis=1)
    bottom = jnp.concatenate([difference[:, 1], -difference[:, 0]], axis=1)
    positions = start + jnp.arange(count, dtype=jnp.int32)
    chosen = jnp.where((positions < M // 2)[:, None], upper_rows, bottom)
    return (chosen * half_root).astype(jnp.bfloat16)


def factor(gram_matrix):
    lower_factor = jnp.linalg.cholesky(gram_matrix)
    identity = jnp.eye(gram_matrix.shape[0], dtype=jnp.float32)
    return jax.scipy.linalg.solve_triangular(lower_factor, identity, lower=True)


def per_device(snapshots, tail_sensors, shift_offsets, start_basis):
    block_rows = snapshots.shape[0]
    row_index = lax.axis_index("row")
    shift_index = lax.axis_index("shift")
    col_count = M // lax.axis_size("shift")
    normalizer = 1.0 / (SNAPS * shift_offsets.shape[0] * lax.axis_size("shift"))
    gathered = lax.all_gather(snapshots, "row", axis=0, tiled=True)
    extended = jnp.concatenate([gathered, tail_sensors], 0)
    every_offset = lax.all_gather(shift_offsets, "shift", axis=0, tiled=True)
    row_start = row_index * block_rows
    col_start = shift_index * col_count

    def add_block(which, running):
        offset = every_offset[which]
        own_rows = make_some(extended, offset, row_start, block_rows)
        col_rows = make_some(extended, offset, col_start, col_count)
        return running + lax.dot_general(
            own_rows, col_rows, (((1,), (1,)), ((), ())), preferred_element_type=jnp.float32
        )

    summed_block = lax.fori_loop(
        0, every_offset.shape[0], add_block, jnp.zeros((block_rows, col_count), jnp.float32)
    )
    cov_out = summed_block * normalizer
    basis_rows = lax.all_gather(start_basis, "row", axis=1, tiled=True)
    own_basis = start_basis
    for sweep in range(ITERS):
        basis_cols = lax.dynamic_slice_in_dim(basis_rows, shift_index * col_count, col_count, 1)
        column_terms = lax.dot_general(
            basis_cols, cov_out, (((1,), (1,)), ((), ())), precision=lax.Precision.HIGHEST
        )
        mapped = lax.psum(column_terms, "shift")
        local_gram = jnp.dot(mapped, mapped.T, precision=lax.Precision.HIGHEST)
        gram_matrix = lax.psum(local_gram, "row")
        own_basis = jnp.dot(factor(gram_matrix), mapped, precision=lax.Precision.HIGHEST)
        if sweep + 1 < ITERS:
            basis_rows = lax.all_gather(own_basis, "row", axis=1, tiled=True)
    return (cov_out, own_basis)


def solution(mesh):
    in_specs = (P("row", None, None), P(), P("shift"), P(None, "row"))
    out_specs = (P("row", "shift"), P(None, "row"))
    return jax.shard_map(
        per_device, mesh=mesh, in_specs=in_specs, out_specs=out_specs, check_vma=False
    )
```

profile of v0, /device:TPU:0, one launch (start us, length us, event | category | flops | bytes accessed | tf_op | source)
XLA Modules:
  0.0 375.3 jit_solution(9196168970584460465)
XLA Ops:
  8.7 1.3 dynamic-slice
  11.5 9.9 %all-reduce = s32[12]{0:T(128)S(1)} all-reduce(s32[12]{0:T(128)S(1)} %dynamic-update-slice.2), channel_id=1, replica_groups=mesh['row'=8,'shift'=4] {'shift'}, use_global_device_ids=true, to_apply=%add | all-reduce | flops 12 | bytes 96
  21.4 19.0 %all-gather.4.cloned.1.call-done = bf16[4096,2,128]{2,1,0:T(2,128)(2,1)} async-done(((bf16[512,2,128]{2,1,0:T(2,128)(2,1)}), bf16[4096,2,128]{2,1,0:T(2,128)(2,1)}) %all-gather.4.cloned.1.call-update) | async-done | bytes 2097168 | tf_op jit(solution)/shard_map/all_gather | solution.py:38
  40.4 6.4 %pad_maximum_fusion = bf16[4224,2,128]{2,1,0:T(2,128)(2,1)S(1)} fusion(bf16[128,2,128]{2,1,0:T(2,128)(2,1)} %param.10, bf16[4096,2,128]{2,1,0:T(2,128)(2,1)} %all-gather.4.cloned.1.call-done), kind=kLoop, calls=%fused_computation.31 | loop fusion | flops 1081344 | bytes 4325376 | tf_op jit(solution)/shard_map/concatenate | solution.py:39
  46.8 1.6 copy.30
  48.4 143.1 %while.18 = (s32[]{:T(128)}, f32[512,1024]{1,0:T(8,128)}, s32[]{:T(128)}, s32[12]{0:T(128)S(1)}, bf16[4224,2,128]{2,0,1:T(8,128)(2,1)}, /*index=5*/s32[]{:T(128)...) while((s32[]{:T(128)}, f32[512,1024]{1,0:T(8,128)}, ...), condition=%wide.region_1.2_spmd.clone, body=%wide.region_0.1_spmd.clone.sunk | while | flops 273222688 | bytes 47713820 | solution.py:52
  52.0 1.2 convert_subtract_fusion.4
  59.1 1.3 copy-done.1
  63.9 1.2 convert_subtract_fusion.4
  65.2 1.2 slice_bitcast_fusion.8
  71.0 1.3 copy-done.1
  75.8 1.2 convert_subtract_fusion.4
  77.1 1.2 slice_bitcast_fusion.8
  82.9 1.3 copy-done.1
  87.8 1.2 convert_subtract_fusion.4
  94.9 1.3 copy-done.1
  99.7 1.2 convert_subtract_fusion.4
  106.8 1.3 copy-done.1
  111.6 1.2 convert_subtract_fusion.4
  118.7 1.3 copy-done.1
  123.5 1.2 convert_subtract_fusion.4
  130.6 1.3 copy-done.1
  135.5 1.2 convert_subtract_fusion.4
  142.6 1.3 copy-done.1
  147.4 1.2 convert_subtract_fusion.4
  154.5 1.3 copy-done.1
  159.3 1.2 convert_subtract_fusion.4
  166.4 1.3 copy-done.1
  171.2 1.2 convert_subtract_fusion.4
  178.3 1.3 copy-done.1
  183.2 1.2 convert_subtract_fusion.4
  190.3 1.3 copy-done.1
  191.6 1.8 broadcast_multiply_fusion
  193.4 4.0 %fusion.16 = f32[64,512]{1,0:T(8,128)} fusion(f32[512,1024]{1,0:T(8,128)S(1)} %broadcast_multiply_fusion, f32[64,4096]{1,0:T(8,128)} %all-gather.6.cloned.1.call-done, s32[]{:T(128)S(6)} %select_n.96), kind=kOutput, calls=%fused_computation.35 | convolution fusion | flops 402653184 | bytes 2490372 | tf_op jit(solution)/shard_map/dot_general | solution.py:60
  197.5 34.7 %all-reduce.4.cloned.1.call-done = f32[64,512]{1,0:T(8,128)} async-done(((f32[64,512]{1,0:T(8,128)}), f32[64,512]{1,0:T(8,128)}) %all-reduce.4.cloned.1.call-update) | async-done | bytes 131088 | tf_op jit(solution)/shard_map/psum | solution.py:63
  232.2 1.2 fusion.32
  233.4 22.4 %psum.29 = f32[64,64]{0,1:T(8,128)S(1)} all-reduce(f32[64,64]{0,1:T(8,128)S(1)} %fusion.32), channel_id=1, replica_groups=mesh['row'=8,'shift'=4] {'row'}, use_global_device_ids=true, to_apply=%region_3.4 | all-reduce | flops 4096 | bytes 32768 | tf_op jit(solution)/shard_map/psum | solution.py:65
  255.9 5.8 %cholesky.44 = f32[64,64]{1,0:T(8,128)S(1)} custom-call(f32[64,64]{1,0:T(8,128)S(1)} %fusion.27), custom_call_target="Cholesky" | custom-call | tf_op jit(solution)/shard_map/jit(cholesky)/cholesky | solution.py:27
  263.1 4.9 %custom-call.7 = f32[1,64,64]{1,2,0:T(8,128)S(1)} custom-call(f32[1,64,64]{2,1,0:T(8,128)S(1)} %fusion.22), custom_call_target="InvertDiagBlocksLowerTriangular" | custom-call | tf_op jit(solution)/shard_map/jit(_solve_triangular)/triangular_solve | solution.py:29
  268.2 1.8 fusion.33
  270.1 22.3 %all-gather.8.cloned.1.call-done = f32[64,4096]{1,0:T(8,128)} async-done(((f32[64,512]{1,0:T(8,128)}), f32[64,4096]{1,0:T(8,128)}) %all-gather.8.cloned.1.call-update) | async-done | bytes 1048592 | tf_op jit(solution)/shard_map/all_gather | solution.py:68
  292.4 3.7 fusion.14
  296.2 34.8 %all-reduce.6.cloned.1.call-done = f32[64,512]{1,0:T(8,128)} async-done(((f32[64,512]{1,0:T(8,128)}), f32[64,512]{1,0:T(8,128)}) %all-reduce.6.cloned.1.call-update) | async-done | bytes 131088 | tf_op jit(solution)/shard_map/psum | solution.py:63
  331.0 1.2 fusion.34
  332.2 22.4 %psum.31 = f32[64,64]{0,1:T(8,128)S(1)} all-reduce(f32[64,64]{0,1:T(8,128)S(1)} %fusion.34), channel_id=1, replica_groups=mesh['row'=8,'shift'=4] {'row'}, use_global_device_ids=true, to_apply=%region_7.10 | all-reduce | flops 4096 | bytes 32768 | tf_op jit(solution)/shard_map/psum | solution.py:65
  354.6 5.8 %cholesky.55 = f32[64,64]{1,0:T(8,128)S(1)} custom-call(f32[64,64]{1,0:T(8,128)S(1)} %fusion.25), custom_call_target="Cholesky" | custom-call | tf_op jit(solution)/shard_map/jit(cholesky)/cholesky | solution.py:27
  361.8 4.9 %custom-call.8 = f32[1,64,64]{1,2,0:T(8,128)S(1)} custom-call(f32[1,64,64]{2,1,0:T(8,128)S(1)} %fusion.23), custom_call_target="InvertDiagBlocksLowerTriangular" | custom-call | tf_op jit(solution)/shard_map/jit(_solve_triangular)/triangular_solve | solution.py:29
  367.0 1.8 fusion.35
  (266 shorter events, 89.9 us)
Async XLA Ops:
  7.2 33.2 %all-gather.4.cloned.1.call-start = ((), (), s32[]{:S(2)}) async-start(), calls=%async_computation | async-start | bytes 2359296 | tf_op jit(solution)/shard_map/all_gather | solution.py:38
  7.9 185.5 %all-gather.6.cloned.1.call-start = ((), (), s32[]{:S(2)}) async-start(), calls=%async_computation.1 | async-start | bytes 1179648 | tf_op jit(solution)/shard_map/all_gather | solution.py:56
  8.6 223.5 %all-reduce.4.cloned.1.call-start = ((), (), s32[]{:S(2)}) async-start(), calls=%async_computation.2 | async-start | bytes 262144 | tf_op jit(solution)/shard_map/psum | solution.py:63
  55.7 2.1 copy-start
  56.5 1.4 copy-start.3
  56.5 1.6 copy-start.4
  59.1 1.3 copy-start.1
  67.6 2.1 copy-start
  68.4 1.4 copy-start.3
  68.4 1.6 copy-start.4
  71.0 1.3 copy-start.1
  79.5 2.1 copy-start
  80.4 1.4 copy-start.3
  80.4 1.6 copy-start.4
  82.9 1.3 copy-start.1
  91.5 2.1 copy-start
  92.3 1.4 copy-start.3
  92.3 1.6 copy-start.4
  94.8 1.3 copy-start.1
  103.4 2.1 copy-start
  104.2 1.4 copy-start.3
  104.2 1.6 copy-start.4
  106.8 1.3 copy-start.1
  115.3 2.1 copy-start
  116.1 1.4 copy-start.3
  116.1 1.6 copy-start.4
  118.7 1.3 copy-start.1
  127.2 2.1 copy-start
  128.1 1.4 copy-start.3
  128.1 1.6 copy-start.4
  139.2 2.1 copy-start
  140.0 1.4 copy-start.3
  140.0 1.6 copy-start.4
  151.1 2.1 copy-start
  151.9 1.4 copy-start.3
  151.9 1.6 copy-start.4
  163.0 2.1 copy-start
  163.8 1.4 copy-start.3
  163.8 1.6 copy-start.4
  174.9 2.1 copy-start
  175.8 1.4 copy-start.3
  175.8 1.6 copy-start.4
  186.9 2.1 copy-start
  187.7 1.4 copy-start.3
  187.7 1.6 copy-start.4
  193.4 102.8 %copy-start.5 = (f32[512,1024]{1,0:T(8,128)}, f32[512,1024]{1,0:T(8,128)S(1)}, u32[]{:S(2)}) copy-start(f32[512,1024]{1,0:T(8,128)S(1)} %broadcast_multiply_fusion) | copy-start | bytes 6291460
  197.4 95.0 %all-gather.8.cloned.1.call-start = ((), (), s32[]{:S(2)}) async-start(), calls=%async_computation.3 | async-start | bytes 1179648 | tf_op jit(solution)/shard_map/all_gather | solution.py:68
  270.1 60.9 %all-reduce.6.cloned.1.call-start = ((), (), s32[]{:S(2)}) async-start(), calls=%async_computation.4 | async-start | bytes 262144 | tf_op jit(solution)/shard_map/psum | solution.py:63
  (18 other events, 23.6 us)
Sparse Core Ops, SparseCore 0:
  9.9 30.4 all-gather.3
  42.3 23.3 all-gather.5
  197.5 34.6 all-reduce.3
  270.2 22.1 all-gather.7
  296.3 34.6 all-reduce.5
where the time goes:
time: 378 us; the launch traced here: 375 us
  waiting for transfers between devices  112 us (30%)
  other arithmetic  102 us (27%)
  blocking collectives  54.6 us (14%)
  local copies, waits for them, and re-layouts  39.1 us (10%)
  loops' own time  26.2 us (7%)
  matrix products  26 us (7%)
  between operations  14.5 us (4%)
    psum x2, waiting for transfers between devices, per_device(): mapped = lax.psum(column_terms, 'shift')  69.5 us
    psum x2, blocking collectives, per_device(): gram_matrix = lax.psum(local_gram, 'row')  44.7 us
    sub x24, other arithmetic, make_some(): difference = window - mirror  28.7 us
    another operation x1, loops' own time, per_device(): lax.fori_loop(0, every_offset.shape[0], add_block, jnp.zeros((block_rows,...  26.2 us
    convert_element_type x24, other arithmetic, make_some(): lax.dynamic_slice_in_dim(extended, offset + M - start - count, count, 0)  26 us
    all_gather x1, waiting for transfers between devices, per_device(): basis_rows = lax.all_gather(own_basis, 'row', axis=1, tiled=True)  22.3 us
    while x120, local copies, waits for them, and re-layouts  19.4 us
    all_gather x1, waiting for transfers between devices, per_device(): gathered = lax.all_gather(snapshots, 'row', axis=0, tiled=True)  19 us
  transfers between devices with their start and end apart: 5, of which 4 were waited for; matrix products, arithmetic and copies ran while one was open for 29% of the time, Pallas kernels for 0%

commit v1 on v0

--- a/solution.py
+++ b/solution.py
@@ -62,7 +62,10 @@
         )
         mapped = lax.psum(column_terms, "shift")
         local_gram = jnp.dot(mapped, mapped.T, precision=lax.Precision.HIGHEST)
-        gram_matrix = lax.psum(local_gram, "row")
+        devices, gram_matrix = (lax.axis_size("row"), local_gram)
+        for hop in [1 << k for k in range(devices.bit_length() - 1)]:
+            swap = [(i, i ^ hop) for i in range(devices)]
+            gram_matrix = gram_matrix + lax.ppermute(gram_matrix, "row", swap)
         own_basis = jnp.dot(factor(gram_matrix), mapped, precision=lax.Precision.HIGHEST)
         if sweep + 1 < ITERS:
             basis_rows = lax.all_gather(own_basis, "row", axis=1, tiled=True)

time: 378 us -> 349 us (0.923)
  blocking collectives: 54.6 us -> 9.92 us
  waiting for transfers between devices: 112 us -> 125 us
  starting transfers between devices: 0.2 us -> 6.33 us
    psum x2 -> x0, blocking collectives: 44.7 us -> none  [per_device(): gram_matrix = lax.psum(local_gram, 'row')]
    ppermute x0 -> x6, waiting for transfers between devices: none -> 12.2 us  [per_device(): gram_matrix = gram_matrix + lax.ppermute(gram_matrix, 'row', swap)]
    ppermute x0 -> x6, starting transfers between devices: none -> 5.95 us  [per_device(): gram_matrix = gram_matrix + lax.ppermute(gram_matrix, 'row', swap)]
  transfers between devices with their start and end apart: 5 -> 11, of which waited for: 4 -> 10; matrix products, arithmetic and copies ran while one was open for 29% -> 32% of each run, Pallas kernels for 0% -> 0%
where the time goes in v1:
time: 349 us; the launch traced here: 347 us
  waiting for transfers between devices  125 us (36%)
  other arithmetic  103 us (30%)
  local copies, waits for them, and re-layouts  38.9 us (11%)
  matrix products  26 us (7%)
  loops' own time  23.5 us (7%)
  between operations  14.6 us (4%)
  blocking collectives  9.92 us (3%)
  starting transfers between devices  6.33 us (2%)
    psum x2, waiting for transfers between devices, per_device(): mapped = lax.psum(column_terms, 'shift')  69.5 us
    sub x24, other arithmetic, make_some(): difference = window - mirror  28.7 us
    convert_element_type x24, other arithmetic, make_some(): lax.dynamic_slice_in_dim(extended, offset + M - start - count, count, 0)  26 us
    another operation x1, loops' own time, per_device(): lax.fori_loop(0, every_offset.shape[0], add_block, jnp.zeros((block_rows,...  23.5 us
    all_gather x1, waiting for transfers between devices, per_device(): basis_rows = lax.all_gather(own_basis, 'row', axis=1, tiled=True)  23 us
    while x120, local copies, waits for them, and re-layouts  19.4 us
    all_gather x1, waiting for transfers between devices, per_device(): gathered = lax.all_gather(snapshots, 'row', axis=0, tiled=True)  18.9 us
    squeeze x24, other arithmetic, make_some(): bottom = jnp.concatenate([difference[:, 1], -difference[:, 0]], axis=1)  15.2 us
  transfers between devices with their start and end apart: 11, of which 10 were waited for; matrix products, arithmetic and copies ran while one was open for 32% of the time, Pallas kernels for 0%

profile of v1, /device:TPU:0, one launch (start us, length us, event | category | flops | bytes accessed | tf_op | source)
XLA Modules:
  0.0 346.9 jit_solution(15807779420143278547)
XLA Ops:
  8.7 1.3 dynamic-slice
  11.6 9.9 %all-reduce = s32[12]{0:T(128)S(1)} all-reduce(s32[12]{0:T(128)S(1)} %dynamic-update-slice.2), channel_id=1, replica_groups=mesh['row'=8,'shift'=4] {'shift'}, use_global_device_ids=true, to_apply=%add | all-reduce | flops 12 | bytes 96
  21.5 18.9 %all-gather.4.cloned.1.call-done = bf16[4096,2,128]{2,1,0:T(2,128)(2,1)} async-done(((bf16[512,2,128]{2,1,0:T(2,128)(2,1)}), bf16[4096,2,128]{2,1,0:T(2,128)(2,1)}) %all-gather.4.cloned.1.call-update) | async-done | bytes 2097168 | tf_op jit(solution)/shard_map/all_gather | solution.py:38
  40.4 6.4 %pad_maximum_fusion = bf16[4224,2,128]{2,1,0:T(2,128)(2,1)S(1)} fusion(bf16[128,2,128]{2,1,0:T(2,128)(2,1)} %param.10, bf16[4096,2,128]{2,1,0:T(2,128)(2,1)} %all-gather.4.cloned.1.call-done), kind=kLoop, calls=%fused_computation.31 | loop fusion | flops 1081344 | bytes 4325376 | tf_op jit(solution)/shard_map/concatenate | solution.py:39
  46.8 1.6 copy.34
  48.4 140.2 %while.18 = (s32[]{:T(128)}, f32[512,1024]{1,0:T(8,128)}, s32[]{:T(128)}, s32[12]{0:T(128)S(1)}, bf16[4224,2,128]{2,0,1:T(8,128)(2,1)}, /*index=5*/s32[]{:T(128)...) while((s32[]{:T(128)}, f32[512,1024]{1,0:T(8,128)}, ...), condition=%wide.region_1.2_spmd.clone, body=%wide.region_0.1_spmd.clone.sunk | while | flops 273222688 | bytes 47713820 | solution.py:52
  51.8 1.2 convert_subtract_fusion.4
  58.8 1.3 copy-done.1
  63.5 1.2 convert_subtract_fusion.4
  70.5 1.3 copy-done.1
  75.2 1.2 convert_subtract_fusion.4
  82.2 1.3 copy-done.1
  86.9 1.2 convert_subtract_fusion.4
  93.9 1.3 copy-done.1
  98.6 1.2 convert_subtract_fusion.4
  105.6 1.3 copy-done.1
  110.3 1.2 convert_subtract_fusion.4
  117.3 1.3 copy-done.1
  121.9 1.2 convert_subtract_fusion.4
  129.0 1.3 copy-done.1
  140.6 1.3 copy-done.1
  152.3 1.3 copy-done.1
  164.0 1.3 copy-done.1
  168.7 1.2 convert_subtract_fusion.4
  175.7 1.3 copy-done.1
  187.4 1.3 copy-done.1
  188.7 1.8 broadcast_multiply_fusion
  190.5 4.0 %fusion.16 = f32[64,512]{1,0:T(8,128)} fusion(f32[512,1024]{1,0:T(8,128)S(1)} %broadcast_multiply_fusion, f32[64,4096]{1,0:T(8,128)} %all-gather.6.cloned.1.call-done, s32[]{:T(128)S(6)} %select_n.96), kind=kOutput, calls=%fused_computation.35 | convolution fusion | flops 402653184 | bytes 2490372 | tf_op jit(solution)/shard_map/dot_general | solution.py:60
  194.6 34.7 %all-reduce.4.cloned.1.call-done = f32[64,512]{1,0:T(8,128)} async-done(((f32[64,512]{1,0:T(8,128)}), f32[64,512]{1,0:T(8,128)}) %all-reduce.4.cloned.1.call-update) | async-done | bytes 131088 | tf_op jit(solution)/shard_map/psum | solution.py:63
  229.3 1.2 fusion.32
  231.8 1.5 collective-permute-start.1
  233.3 2.5 collective-permute-done.1
  235.8 1.5 collective-permute-start.2
  237.2 2.5 collective-permute-done.2
  239.8 5.8 %cholesky.44 = f32[64,64]{1,0:T(8,128)S(1)} custom-call(f32[64,64]{1,0:T(8,128)S(1)} %fusion.27), custom_call_target="Cholesky" | custom-call | tf_op jit(solution)/shard_map/jit(cholesky)/cholesky | solution.py:27
  247.0 4.9 %custom-call.7 = f32[1,64,64]{1,2,0:T(8,128)S(1)} custom-call(f32[1,64,64]{2,1,0:T(8,128)S(1)} %fusion.22), custom_call_target="InvertDiagBlocksLowerTriangular" | custom-call | tf_op jit(solution)/shard_map/jit(_solve_triangular)/triangular_solve | solution.py:29
  252.1 1.8 fusion.33
  254.2 23.0 %all-gather.8.cloned.1.call-done = f32[64,4096]{1,0:T(8,128)} async-done(((f32[64,512]{1,0:T(8,128)}), f32[64,4096]{1,0:T(8,128)}) %all-gather.8.cloned.1.call-update) | async-done | bytes 1048592 | tf_op jit(solution)/shard_map/all_gather | solution.py:71
  277.2 3.7 %fusion.14 = f32[64,512]{1,0:T(8,128)} fusion(f32[512,1024]{1,0:T(8,128)S(1)} %broadcast_multiply_fusion, f32[64,4096]{1,0:T(8,128)} %all-gather.8.cloned.1.call-done, s32[]{:T(128)S(6)} %select_n.96), kind=kOutput, calls=%fused_computation.33 | convolution fusion | flops 402653184 | bytes 2490372 | tf_op jit(solution)/shard_map/dot_general | solution.py:60
  280.9 34.8 %all-reduce.6.cloned.1.call-done = f32[64,512]{1,0:T(8,128)} async-done(((f32[64,512]{1,0:T(8,128)}), f32[64,512]{1,0:T(8,128)}) %all-reduce.6.cloned.1.call-update) | async-done | bytes 131088 | tf_op jit(solution)/shard_map/psum | solution.py:63
  315.7 1.2 fusion.34
  318.3 1.4 collective-permute-start.4
  319.7 2.5 collective-permute-done.4
  322.2 1.5 collective-permute-start.5
  323.6 2.5 collective-permute-done.5
  326.2 5.8 %cholesky.55 = f32[64,64]{1,0:T(8,128)S(1)} custom-call(f32[64,64]{1,0:T(8,128)S(1)} %fusion.25), custom_call_target="Cholesky" | custom-call | tf_op jit(solution)/shard_map/jit(cholesky)/cholesky | solution.py:27
  333.4 4.9 %custom-call.8 = f32[1,64,64]{1,2,0:T(8,128)S(1)} custom-call(f32[1,64,64]{2,1,0:T(8,128)S(1)} %fusion.23), custom_call_target="InvertDiagBlocksLowerTriangular" | custom-call | tf_op jit(solution)/shard_map/jit(_solve_triangular)/triangular_solve | solution.py:29
  338.6 1.8 fusion.35
  (282 shorter events, 99.7 us)
Async XLA Ops:
  7.2 33.2 %all-gather.4.cloned.1.call-start = ((), (), s32[]{:S(2)}) async-start(), calls=%async_computation | async-start | bytes 2359296 | tf_op jit(solution)/shard_map/all_gather | solution.py:38
  7.9 182.6 %all-gather.6.cloned.1.call-start = ((), (), s32[]{:S(2)}) async-start(), calls=%async_computation.1 | async-start | bytes 1179648 | tf_op jit(solution)/shard_map/all_gather | solution.py:56
  8.6 220.7 %all-reduce.4.cloned.1.call-start = ((), (), s32[]{:S(2)}) async-start(), calls=%async_computation.2 | async-start | bytes 262144 | tf_op jit(solution)/shard_map/psum | solution.py:63
  55.5 2.0 copy-start
  56.3 1.4 copy-start.3
  56.3 1.6 copy-start.4
  67.2 2.0 copy-start
  68.0 1.4 copy-start.3
  68.0 1.6 copy-start.4
  78.9 2.0 copy-start
  79.6 1.4 copy-start.3
  79.7 1.6 copy-start.4
  90.6 2.0 copy-start
  91.3 1.4 copy-start.3
  91.3 1.6 copy-start.4
  102.3 2.0 copy-start
  103.0 1.4 copy-start.3
  103.0 1.6 copy-start.4
  114.0 2.0 copy-start
  114.7 1.4 copy-start.3
  114.7 1.6 copy-start.4
  125.6 2.0 copy-start
  126.4 1.4 copy-start.3
  126.4 1.6 copy-start.4
  137.3 2.0 copy-start
  138.1 1.4 copy-start.3
  138.1 1.6 copy-start.4
  149.0 2.0 copy-start
  149.7 1.4 copy-start.3
  149.8 1.6 copy-start.4
  160.7 2.0 copy-start
  161.4 1.4 copy-start.3
  161.4 1.6 copy-start.4
  172.4 2.0 copy-start
  173.1 1.4 copy-start.3
  173.1 1.6 copy-start.4
  184.1 2.0 copy-start
  184.8 1.4 copy-start.3
  184.8 1.6 copy-start.4
  190.5 90.4 %copy-start.5 = (f32[512,1024]{1,0:T(8,128)}, f32[512,1024]{1,0:T(8,128)S(1)}, u32[]{:S(2)}) copy-start(f32[512,1024]{1,0:T(8,128)S(1)} %broadcast_multiply_fusion) | copy-start | bytes 6291460
  194.5 82.7 %all-gather.8.cloned.1.call-start = ((), (), s32[]{:S(2)}) async-start(), calls=%async_computation.3 | async-start | bytes 1179648 | tf_op jit(solution)/shard_map/all_gather | solution.py:71
  230.6 1.3 collective-permute-start
  231.8 3.9 %collective-permute-start.1 = (f32[64,64]{0,1:T(8,128)S(1)}, f32[64,64]{0,1:T(8,128)S(1)}, u32[]{:S(2)}, u32[]{:S(2)}) collective-permute-start(f32[64,64]{0,1:T(8,128)S(1)} %add.269), channel_id=1, source_target_pairs={{0,8},{4,12},{8,0},{12,4},{16,24},{20,28},{24,16},{28,20},{1,9},{5... | collective-permute-start | bytes 49160 | tf_op jit(solution)/shard_map/ppermute | solution.py:68
  235.8 3.9 %collective-permute-start.2 = (f32[64,64]{0,1:T(8,128)S(1)}, f32[64,64]{0,1:T(8,128)S(1)}, u32[]{:S(2)}, u32[]{:S(2)}) collective-permute-start(f32[64,64]{0,1:T(8,128)S(1)} %add.270), channel_id=1, source_target_pairs={{0,16},{4,20},{8,24},{12,28},{16,0},{20,4},{24,8},{28,12},{1,17},{... | collective-permute-start | bytes 49160 | tf_op jit(solution)/shard_map/ppermute | solution.py:68
  254.0 61.8 %all-reduce.6.cloned.1.call-start = ((), (), s32[]{:S(2)}) async-start(), calls=%async_computation.4 | async-start | bytes 262144 | tf_op jit(solution)/shard_map/psum | solution.py:63
  317.0 1.3 collective-permute-start.3
  318.3 3.9 %collective-permute-start.4 = (f32[64,64]{0,1:T(8,128)S(1)}, f32[64,64]{0,1:T(8,128)S(1)}, u32[]{:S(2)}, u32[]{:S(2)}) collective-permute-start(f32[64,64]{0,1:T(8,128)S(1)} %add.272), channel_id=1, source_target_pairs={{0,8},{4,12},{8,0},{12,4},{16,24},{20,28},{24,16},{28,20},{1,9},{5... | collective-permute-start | bytes 49160 | tf_op jit(solution)/shard_map/ppermute | solution.py:68
  322.2 3.9 %collective-permute-start.5 = (f32[64,64]{0,1:T(8,128)S(1)}, f32[64,64]{0,1:T(8,128)S(1)}, u32[]{:S(2)}, u32[]{:S(2)}) collective-permute-start(f32[64,64]{0,1:T(8,128)S(1)} %add.273), channel_id=1, source_target_pairs={{0,16},{4,20},{8,24},{12,28},{16,0},{20,4},{24,8},{28,12},{1,17},{... | collective-permute-start | bytes 49160 | tf_op jit(solution)/shard_map/ppermute | solution.py:68
  (24 other events, 31.5 us)
Sparse Core Ops, SparseCore 0:
  9.9 30.4 all-gather.3
  42.3 23.3 all-gather.5
  194.6 34.6 all-reduce.3
  254.1 23.0 all-gather.7
  281.1 34.6 all-reduce.5
